TPU v7x, 32 devices: a whole 2x2x4 slice. The times are simulated.
32 devices in a mesh: batch: 4 (over x, core), lat: 8 (over z, y).
Axes of the slice: x: 2, y: 2, z: 4, core: 2. Of those that a mesh axis runs over, the one named last changes fastest.
Arguments:
- predicted: bfloat16 [4, 73, 192, 1440], P('batch', None, 'lat'), may hold values from -64 to 64
- target: bfloat16 [4, 73, 192, 1440], P('batch', None, 'lat'), may hold values from -128 to 128
- legendre_basis: bfloat16 [192, 96, 720], P(None, ('batch', 'lat')), may hold values from -1 to 1
Outputs:
- spectra: float32 [2, 73, 720], replicated
- channel_loss: float32 [73], replicated
All inputs are finite; a program needn't handle non-finite values.
Results may differ from a plain program's by a relative error of at most 0.0003.
Values may be sent and summed in bfloat16 or wider, within the bound.
A program may use at most 128 MiB of HBM per device.

v0:
```python
import math

import jax
import jax.numpy as jnp
from jax import lax
from jax.sharding import PartitionSpec as P


def fourier_table(lon_count, order_count):
    lon_ids = jnp.arange(lon_count, dtype=jnp.int32)
    order_ids = jnp.arange(order_count, dtype=jnp.int32)
    product_ids = lon_ids[:, None] * order_ids[None, :] % lon_count
    angles = 2.0 * math.pi / lon_count * product_ids.astype(jnp.float32)
    inv_root = 1.0 / math.sqrt(lon_count)
    return jnp.stack([jnp.cos(angles) * inv_root, -jnp.sin(angles) * inv_root], axis=1).astype(
        jnp.bfloat16
    )


def band_energy(fourier, basis_block, orders):
    coefficients = jnp.einsum(
        "fpmbcn,nml->fpmbcl", fourier, basis_block, preferred_element_type=jnp.float32
    )
    squares = jnp.sum(coefficients * coefficients, axis=1)
    weights = jnp.where(orders == 0, 1.0, 2.0).astype(jnp.float32)
    return jnp.sum(squares * weights[None, :, None, None, None], axis=(1, 2))


def body(predicted, target, legendre_basis):
    groups = lax.axis_size("batch")
    band_count = lax.axis_size("lat")
    per_dev = legendre_basis.shape[1]
    order_count = per_dev * groups * band_count
    dft_table = fourier_table(predicted.shape[3], order_count)
    band_id = lax.axis_index("lat")

    def transform(field_in):
        return jnp.einsum(
            "bcnk,kpm->pmbcn", field_in, dft_table, preferred_element_type=jnp.float32
        ).astype(jnp.bfloat16)

    fourier = jnp.stack([transform(predicted), transform(target)], axis=0)
    members = fourier.shape[3]
    channels = fourier.shape[4]
    lat_rows = fourier.shape[5]
    fourier = fourier.reshape(2, 2, groups, band_count, per_dev, members, channels, lat_rows)
    arrived = lax.all_to_all(fourier, "lat", split_axis=3, concat_axis=7, tiled=True)
    arrived = arrived.reshape(
        2, 2, groups * per_dev, arrived.shape[5], arrived.shape[6], arrived.shape[7]
    )
    basis_block = lax.all_gather(legendre_basis, "batch", axis=1, tiled=True)
    taken = basis_block.shape[1]
    gathered_ids = jnp.arange(taken, dtype=jnp.int32)
    orders = (
        gathered_ids // per_dev * band_count * per_dev + band_id * per_dev + gathered_ids % per_dev
    )
    partial_value = band_energy(arrived, basis_block, orders)
    energy = lax.psum(partial_value, "lat")
    energy = lax.psum(energy, "batch")
    spectra = energy / (predicted.shape[0] * groups * order_count)
    log_spectra = jnp.log(spectra + 1e-06)
    channel_loss = jnp.mean((log_spectra[0] - log_spectra[1]) ** 2, axis=1)
    return (spectra, channel_loss)


def solution(mesh):
    placed = (
        P("batch", None, "lat", None),
        P("batch", None, "lat", None),
        P(None, ("batch", "lat"), None),
    )
    return jax.shard_map(body, mesh=mesh, in_specs=placed, out_specs=(P(), P()), check_vma=False)
```

profile of v0, /device:TPU:0, one launch (start us, length us, event | category | flops | bytes accessed | tf_op | source)
XLA Modules:
  0.0 212.2 jit_solution(11625327290755649896)
XLA Ops:
  7.2 0.0 all-gather.2.cloned.1.call-start
  7.2 0.7 all-gather.2.cloned.1.call-update
  7.9 2.6 %multiply_convert_fusion = (bf16[1440,1,96]{0,2,1:T(8,128)(2,1)S(1)}, bf16[1440,1,96]{0,2,1:T(8,128)(2,1)S(1)}) fusion(), kind=kLoop, calls=%fused_computation.17 | loop fusion | flops 1935360 | bytes 552960 | tf_op jit(solution)/shard_map/convert.1
  10.5 0.0 copy-start
  10.5 0.0 copy-start.1
  10.5 0.7 copy-done
  11.2 0.1 copy-done.1
  11.3 4.8 %fusion.8 = bf16[2,96,73,24]{1,2,3,0:T(8,128)(2,1)S(1)} fusion(bf16[73,24,1440]{2,1,0:T(8,128)(2,1)} %bitcast.33, bf16[1440,1,96]{0,2,1:T(8,128)(2,1)S(1)} %get-tuple-element.4, bf16[1440,1,96]{0,2,1:T(8,128)(2,1)S(1)} %get-tuple-element.5), kind=kOutput, calls=%fused_computation.11 | convolution fusion | flops 970228224 | bytes 6271488 | tf_op jit(solution)/shard_map/bcnk,kpm->pmbcn/dot_general | solution.py:38
  16.1 0.9 copy.29
  17.0 5.5 %fusion.11 = bf16[2,96,73,24]{1,2,3,0:T(8,128)(2,1)S(1)} fusion(bf16[73,24,1440]{2,1,0:T(8,128)(2,1)} %bitcast.34, bf16[1440,1,96]{0,2,1:T(8,128)(2,1)} %copy-done, bf16[1440,1,96]{0,2,1:T(8,128)(2,1)} %copy-done.1), kind=kOutput, calls=%fused_computation.12 | convolution fusion | flops 970228224 | bytes 6271488 | tf_op jit(solution)/shard_map/bcnk,kpm->pmbcn/dot_general | solution.py:38
  22.5 0.9 copy.31
  23.3 0.5 pad_maximum_fusion
  23.9 2.0 copy.32
  25.9 7.5 %all-to-all-start = ((bf16[2,2,4,8,3,1,73,24]{6,7,4,2,1,5,0,3:T(8,128)(2,1)}), bf16[2,2,4,8,3,1,73,24]{6,7,4,2,1,5,0,3:T(8,128)(2,1)S(1)}, u32[]{:S(2)}, u32[]{:S(2)}) async-start(bf16[2,2,4,8,3,1,73,24]{6,7,4,2,1,5,0,3:T(8,128)(2,1)} %copy.32), calls=%async_computation | async-start | bytes 4718592 | tf_op jit(solution)/shard_map/all_to_all | solution.py:47
  33.5 0.0 all-reduce.3.cloned.1.call-start
  33.5 53.6 %all-to-all-done = bf16[2,2,4,8,3,1,73,24]{6,7,4,2,1,5,0,3:T(8,128)(2,1)S(1)} async-done(((bf16[2,2,4,8,3,1,73,24]{6,7,4,2,1,5,0,3:T(8,128)(2,1)}), bf16[2,2,4,8,3,1,73,24]{6,7,4,2,1,5,0,3:T(8,128)(2,1)S(1)}, u32[]{:S(2)}, u32[]{:S(2)}) %all-to-all-start) | async-done | bytes 1345568 | tf_op jit(solution)/shard_map/all_to_all | solution.py:47
  87.1 2.1 copy.33
  89.2 0.0 all-gather.2.cloned.1.call-done
  89.2 5.1 %multiply_reduce_fusion = f32[12,2,73,720]{3,2,1,0:T(8,128)S(1)} fusion(bf16[192,12,720]{2,0,1:T(8,128)(2,1)} %all-gather.2.cloned.1.call-done, bf16[2,2,12,73,192]{3,4,2,1,0:T(8,128)(2,1)} %bitcast.30), kind=kOutput, calls=%fused_computation | convolution fusion | flops 972570240 | bytes 9709056 | tf_op jit(solution)/shard_map/fpmbcn,nml->fpmbcl/dot_general | solution.py:21
  94.3 0.6 multiply_reduce_fusion.1
  94.9 1.1 copy.40
  96.0 0.0 all-reduce.3.cloned.1.call-update
  96.1 0.0 all-reduce.5.cloned.1.call-start
  96.1 71.4 %all-reduce.3.cloned.1.call-done = f32[2,73,720]{2,0,1:T(2,128)} async-done(((f32[2,73,720]{2,0,1:T(2,128)}), f32[2,73,720]{2,0,1:T(2,128)}) %all-reduce.3.cloned.1.call-update) | async-done | bytes 420496 | tf_op jit(solution)/shard_map/psum | solution.py:58
  167.5 0.0 all-reduce.5.cloned.1.call-update
  167.6 34.7 %all-reduce.5.cloned.1.call-done = f32[2,73,720]{2,0,1:T(2,128)} async-done(((f32[2,73,720]{2,0,1:T(2,128)}), f32[2,73,720]{2,0,1:T(2,128)}) %all-reduce.5.cloned.1.call-update) | async-done | bytes 420496 | tf_op jit(solution)/shard_map/psum | solution.py:59
  202.2 2.2 %add_log_fusion = (f32[2,73,720]{2,0,1:T(2,128)S(1)}, f32[2,73,720]{2,0,1:T(2,128)}) fusion(f32[2,73,720]{2,0,1:T(2,128)} %all-reduce.5.cloned.1.call-done), kind=kLoop, calls=%fused_computation.23 | loop fusion | flops 210240 | bytes 1261440 | tf_op jit(solution)/shard_map/log | solution.py:61
  204.5 0.6 fusion.20
  205.1 0.5 broadcast_multiply_fusion.1
  (1 shorter events, 0.0 us)
Async XLA Ops:
  7.2 82.1 %all-gather.2.cloned.1.call-start = ((), (), s32[]{:S(2)}) async-start(), calls=%async_computation.1 | async-start | bytes 4423680 | tf_op jit(solution)/shard_map/all_gather | solution.py:51
  10.5 0.7 copy-start
  10.5 0.8 copy-start.1
  25.9 61.2 %all-to-all-start = ((bf16[2,2,4,8,3,1,73,24]{6,7,4,2,1,5,0,3:T(8,128)(2,1)}), bf16[2,2,4,8,3,1,73,24]{6,7,4,2,1,5,0,3:T(8,128)(2,1)S(1)}, u32[]{:S(2)}, u32[]{:S(2)}) async-start(bf16[2,2,4,8,3,1,73,24]{6,7,4,2,1,5,0,3:T(8,128)(2,1)} %copy.32), calls=%async_computation | async-start | bytes 4718592 | tf_op jit(solution)/shard_map/all_to_all | solution.py:47
  33.5 134.1 %all-reduce.3.cloned.1.call-start = ((), (), s32[]{:S(2)}) async-start(), calls=%async_computation.2 | async-start | bytes 897024 | tf_op jit(solution)/shard_map/psum | solution.py:58
  96.1 106.2 %all-reduce.5.cloned.1.call-start = ((), (), s32[]{:S(2)}) async-start(), calls=%async_computation.3 | async-start | bytes 897024 | tf_op jit(solution)/shard_map/psum | solution.py:59
Sparse Core Ops, SparseCore 0:
  9.5 33.4 all-gather.1
  96.2 71.2 all-reduce.2
  169.9 32.2 all-reduce.4
where the time goes:
time: 212 us
  waiting for transfers between devices  160 us (75%)
  matrix products  15.4 us (7%)
  between operations  13.8 us (7%)
  local copies, waits for them, and re-layouts  7.77 us (4%)
  starting transfers between devices  7.66 us (4%)
  other arithmetic  7.07 us (3%)
    psum x1, waiting for transfers between devices, body(): energy = lax.psum(partial_value, 'lat')  71.4 us
    all_to_all x1, waiting for transfers between devices, body(): lax.all_to_all(fourier, 'lat', split_axis=3, concat_axis=7, tiled=True)  53.6 us
    psum x1, waiting for transfers between devices, body(): energy = lax.psum(energy, 'batch')  34.7 us
    dot_general x2, matrix products, transform(): jnp.einsum('bcnk,kpm->pmbcn', field_in, dft_table, preferred_element_type...  10.3 us
    all_to_all x1, starting transfers between devices, body(): lax.all_to_all(fourier, 'lat', split_axis=3, concat_axis=7, tiled=True)  7.55 us
    dot_general x1, matrix products, band_energy(): jnp.einsum('fpmbcn,nml->fpmbcl', fourier, basis_block, preferred_element_...  5.1 us
  transfers between devices with their start and end apart: 4, of which 3 were waited for; matrix products, arithmetic and copies ran while one was open for 9% of the time, Pallas kernels for 0%

commit v1 on v0

v1 whole, which is shorter than its diff:
```python
import functools
import math

import jax
import jax.numpy as jnp
import numpy as np
from jax import lax
from jax.experimental import pallas as pl
from jax.experimental.pallas import tpu as pltpu
from jax.sharding import PartitionSpec as P

MESH = pl.DeviceIdType.MESH
VMEM_SPEC = pl.BlockSpec(memory_space=pltpu.VMEM)


def fourier_table(lon_count, order_count):
    product_ids = np.arange(lon_count)[:, None] * np.arange(order_count)[None, :] % lon_count
    angles = np.float32(2.0 * math.pi / lon_count) * product_ids.astype(np.float32)
    inv_root = np.float32(1.0 / math.sqrt(lon_count))
    table = np.stack([np.cos(angles) * inv_root, -np.sin(angles) * inv_root], axis=2)
    return table.astype(jnp.bfloat16)


def greet_all(groups, bands):
    count = groups * bands
    me = lax.axis_index("batch") * bands + lax.axis_index("lat")
    barrier = pltpu.get_barrier_semaphore()

    @pl.loop(1, count)
    def _(step):
        peer = lax.rem(me + step, count)
        pl.semaphore_signal(
            barrier, inc=1, device_id=(peer // bands, lax.rem(peer, bands)), device_id_type=MESH
        )

    pl.semaphore_wait(barrier, count - 1)


def exchange_kernel(groups, bands, send_ref, recv_ref, send_sem, recv_sem):
    count = groups * bands
    me = lax.axis_index("batch") * bands + lax.axis_index("lat")
    greet_all(groups, bands)

    def copy_to(peer, slot):
        return pltpu.make_async_remote_copy(
            src_ref=send_ref.at[peer],
            dst_ref=recv_ref.at[slot],
            send_sem=send_sem.at[peer],
            recv_sem=recv_sem.at[slot],
            device_id=(peer // bands, lax.rem(peer, bands)),
            device_id_type=MESH,
        )

    @pl.loop(1, count)
    def _(step):
        copy_to(lax.rem(me + step, count), me).start()

    recv_ref[me] = send_ref[me]

    @pl.loop(1, count)
    def _(step):
        peer = lax.rem(me + step, count)
        copy_to(peer, peer).wait_recv()
        copy_to(peer, peer).wait_send()


def exchange(groups, bands, blocks):
    count = groups * bands
    return pl.pallas_call(
        functools.partial(exchange_kernel, groups, bands),
        out_shape=jax.ShapeDtypeStruct(blocks.shape, blocks.dtype),
        in_specs=[VMEM_SPEC],
        out_specs=VMEM_SPEC,
        scratch_shapes=[pltpu.SemaphoreType.DMA((count,)), pltpu.SemaphoreType.DMA((count,))],
        compiler_params=pltpu.CompilerParams(collective_id=0, has_side_effects=True),
    )(blocks)


def total_kernel(groups, bands, part_ref, out_ref, first, second, mid, sems):
    my_group = lax.axis_index("batch")
    my_band = lax.axis_index("lat")
    greet_all(groups, bands)

    def over(axis_size, mine, make):
        @pl.loop(1, axis_size)
        def _(step):
            make(lax.rem(mine + step, axis_size), mine).start()

    def finish(axis_size, mine, make):
        @pl.loop(1, axis_size)
        def _(step):
            peer = lax.rem(mine + step, axis_size)
            make(peer, peer).wait_recv()
            make(peer, peer).wait_send()

    def scatter_groups(peer, slot):
        return pltpu.make_async_remote_copy(
            src_ref=part_ref.at[peer], dst_ref=first.at[slot],
            send_sem=sems.at[0, peer], recv_sem=sems.at[1, slot],
            device_id=(peer, my_band), device_id_type=MESH,
        )

    def scatter_bands(peer, slot):
        return pltpu.make_async_remote_copy(
            src_ref=mid.at[peer], dst_ref=second.at[slot],
            send_sem=sems.at[2, peer], recv_sem=sems.at[3, slot],
            device_id=(my_group, peer), device_id_type=MESH,
        )

    def gather_bands(peer, slot):
        return pltpu.make_async_remote_copy(
            src_ref=out_ref.at[my_group, my_band], dst_ref=out_ref.at[my_group, slot],
            send_sem=sems.at[4, peer], recv_sem=sems.at[5, slot],
            device_id=(my_group, peer), device_id_type=MESH,
        )

    def gather_groups(peer, slot):
        return pltpu.make_async_remote_copy(
            src_ref=out_ref.at[my_group], dst_ref=out_ref.at[slot],
            send_sem=sems.at[6, peer], recv_sem=sems.at[7, slot],
            device_id=(peer, my_band), device_id_type=MESH,
        )

    over(groups, my_group, scatter_groups)
    first[my_group] = part_ref[my_group]
    finish(groups, my_group, scatter_groups)
    mid[...] = jnp.sum(first[...], axis=0)

    over(bands, my_band, scatter_bands)
    second[my_band] = mid[my_band]
    finish(bands, my_band, scatter_bands)
    out_ref[my_group, my_band] = jnp.sum(second[...], axis=0)

    over(bands, my_band, gather_bands)
    finish(bands, my_band, gather_bands)
    over(groups, my_group, gather_groups)
    finish(groups, my_group, gather_groups)


def total(groups, bands, part):
    widest = max(groups, bands)
    tile = part.shape[2:]
    return pl.pallas_call(
        functools.partial(total_kernel, groups, bands),
        out_shape=jax.ShapeDtypeStruct(part.shape, part.dtype),
        in_specs=[VMEM_SPEC],
        out_specs=VMEM_SPEC,
        scratch_shapes=[
            pltpu.VMEM((groups, bands) + tile, jnp.float32),
            pltpu.VMEM((bands,) + tile, jnp.float32),
            pltpu.VMEM((bands,) + tile, jnp.float32),
            pltpu.SemaphoreType.DMA((8, widest)),
        ],
        compiler_params=pltpu.CompilerParams(collective_id=1, has_side_effects=True),
    )(part)


def body(predicted, target, legendre_basis):
    groups = lax.axis_size("batch")
    bands = lax.axis_size("lat")
    count = groups * bands
    lat_total, per_dev, degrees = legendre_basis.shape
    members, channels, lat_rows, lon_count = predicted.shape
    order_count = per_dev * count
    table = jnp.asarray(fourier_table(lon_count, order_count))
    table = table.reshape(lon_count, count, per_dev, 2)

    def transform(field_in):
        return jnp.einsum(
            "bcnk,kdmp->dmpbnc", field_in, table, preferred_element_type=jnp.float32
        ).astype(jnp.bfloat16)

    blocks = jnp.stack([transform(predicted), transform(target)], axis=2)
    blocks = blocks.transpose(0, 4, 5, 1, 2, 3, 6).reshape(count, members * lat_rows, -1)
    arrived = exchange(groups, bands, blocks)
    arrived = arrived.reshape(groups, bands, members, lat_rows, per_dev, 2, 2, channels)
    basis = legendre_basis.reshape(bands, lat_rows, per_dev, degrees)
    coefficients = jnp.einsum(
        "gtbnmfpc,tnml->mgbpfcl", arrived, basis, preferred_element_type=jnp.float32
    )
    me = lax.axis_index("batch") * bands + lax.axis_index("lat")
    orders = me * per_dev + jnp.arange(per_dev, dtype=jnp.int32)
    weights = jnp.where(orders == 0, 1.0, 2.0).astype(jnp.float32)
    weights = weights[:, None, None, None, None, None, None]
    part = jnp.sum(coefficients * coefficients * weights, axis=(0, 1, 2, 3))

    rows = 2 * channels
    row_tiles, lane_tiles = -(-rows // 8), -(-degrees // 128)
    tiles = row_tiles * lane_tiles
    per_chunk = -(-tiles // count)
    part = jnp.pad(
        part.reshape(rows, degrees), ((0, row_tiles * 8 - rows), (0, lane_tiles * 128 - degrees))
    )
    part = part.reshape(row_tiles, 8, lane_tiles, 128).transpose(0, 2, 1, 3)
    part = jnp.pad(part.reshape(tiles, 8, 128), ((0, per_chunk * count - tiles), (0, 0), (0, 0)))
    energy = total(groups, bands, part.reshape(groups, bands, per_chunk, 8, 128))
    energy = energy.reshape(per_chunk * count, 8, 128)[:tiles]
    energy = energy.reshape(row_tiles, lane_tiles, 8, 128).transpose(0, 2, 1, 3)
    energy = energy.reshape(row_tiles * 8, lane_tiles * 128)[:rows, :degrees]
    energy = energy.reshape(2, channels, degrees)

    spectra = energy / (members * groups * order_count)
    log_spectra = jnp.log(spectra + 1e-06)
    channel_loss = jnp.mean((log_spectra[0] - log_spectra[1]) ** 2, axis=1)
    return (spectra, channel_loss)


def solution(mesh):
    placed = (
        P("batch", None, "lat", None),
        P("batch", None, "lat", None),
        P(None, ("batch", "lat"), None),
    )
    return jax.shard_map(body, mesh=mesh, in_specs=placed, out_specs=(P(), P()), check_vma=False)
```

time: 212 us -> 101 us (0.48)
  waiting for transfers between devices: 160 us -> 0 us
  Pallas kernels: 0 us -> 68.7 us
  between operations: 13.8 us -> 0.76 us
  local copies, waits for them, and re-layouts: 7.77 us -> 17.2 us
  starting transfers between devices: 7.66 us -> 0 us
  other arithmetic: 7.07 us -> 1.29 us
  matrix products: 15.4 us -> 11.4 us
    psum x2 -> x0, waiting for transfers between devices: 106 us -> none  [the longest x1 71.4 us: body(): energy = lax.psum(partial_value, 'lat')]
    pallas_call x0 -> x2, Pallas kernels: none -> 68.7 us  [the longest x1 38.8 us: exchange(): pl.pallas_call(functools.partial(exchange_kernel, groups, bands), out_sha...]
    all_to_all x1 -> x0, waiting for transfers between devices: 53.6 us -> none  [body(): lax.all_to_all(fourier, 'lat', split_axis=3, concat_axis=7, tiled=True)]
    all_to_all x1 -> x0, starting transfers between devices: 7.55 us -> none  [body(): lax.all_to_all(fourier, 'lat', split_axis=3, concat_axis=7, tiled=True)]
    another operation x1, local copies, waits for them, and re-layouts: 2.04 us -> 6.82 us  [body(): fourier = jnp.stack([transform(predicted), transform(target)], axis=0)]
    dot_general x3, matrix products: 15.4 us -> 11.4 us  [the longest x2 8.21 us: transform(): jnp.einsum('bcnk,kdmp->dmpbnc', field_in, table, preferred_element_type=j...]
    reshape x0 -> x2, local copies, waits for them, and re-layouts: none -> 3.75 us  [the longest x1 2.67 us: body(): blocks.transpose(0, 4, 5, 1, 2, 3, 6).reshape(count, members * lat_rows, -1)]
    another operation x2 -> x0, other arithmetic: 3.1 us -> none
  transfers between devices with their start and end apart: 4 -> 0, of which waited for: 3 -> 0; matrix products, arithmetic and copies ran while one was open for 9% -> 0% of each run, Pallas kernels for 0% -> 0%
where the time goes in v1:
time: 101 us; the launch traced here: 99.4 us
  Pallas kernels  68.7 us (68%)
  local copies, waits for them, and re-layouts  17.2 us (17%)
  matrix products  11.4 us (11%)
  other arithmetic  1.29 us (1%)
    pallas_call x1, Pallas kernels, exchange(): pl.pallas_call(functools.partial(exchange_kernel, groups, bands), out_sha...  38.8 us
    pallas_call x1, Pallas kernels, total(): pl.pallas_call(functools.partial(total_kernel, groups, bands), out_shape=...  29.9 us
    dot_general x2, matrix products, transform(): jnp.einsum('bcnk,kdmp->dmpbnc', field_in, table, preferred_element_type=j...  8.21 us
    another operation x1, local copies, waits for them, and re-layouts  6.82 us
    dot_general x1, matrix products, body(): jnp.einsum('gtbnmfpc,tnml->mgbpfcl', arrived, basis, preferred_element_ty...  3.18 us
    reshape x1, local copies, waits for them, and re-layouts, body(): blocks.transpose(0, 4, 5, 1, 2, 3, 6).reshape(count, members * lat_rows, -1)  2.67 us
    transpose x1, local copies, waits for them, and re-layouts, body(): blocks.transpose(0, 4, 5, 1, 2, 3, 6).reshape(count, members * lat_rows, -1)  2.43 us
    unnamed x7, local copies, waits for them, and re-layouts  2.27 us

profile of v1, /device:TPU:0, one launch (start us, length us, event | category | flops | bytes accessed | tf_op | source)
XLA Modules:
  0.0 99.4 jit_solution(4260858847240235929)
XLA Ops:
  0.6 0.0 copy-start
  0.7 1.1 %copy-done = bf16[192,3,720]{2,0,1:T(8,128)(2,1)S(1)} copy-done((bf16[192,3,720]{2,0,1:T(8,128)(2,1)S(1)}, bf16[192,3,720]{2,0,1:T(8,128)(2,1)}, u32[]{:S(2)}) %copy-start) | copy-done | bytes 829464
  1.8 0.0 copy-start.1
  1.8 0.0 copy-start.2
  1.8 5.5 %fusion.15 = bf16[32,3,1,2,1,24,73]{6,0,5,3,1,4,2:T(8,128)(2,1)S(1)} fusion(bf16[1440,32,3,2,1]{0,1,4,3,2:T(8,128)(2,1)} %constant.41, bf16[73,24,1440,1,1]{2,1,0,4,3:T(8,128)(2,1)} %bitcast.63), kind=kOutput, calls=%fused_computation.12 | convolution fusion | flops 969122304 | bytes 6271488 | tf_op jit(solution)/shard_map/bcnk,kdmp->dmpbnc/dot_general | solution.py:169
  7.3 0.0 copy-done.1
  7.3 0.0 copy-done.2
  7.3 2.7 %fusion.12 = bf16[32,3,1,2,1,24,73]{6,0,5,3,1,4,2:T(8,128)(2,1)S(1)} fusion(bf16[1440,32,3,2,1]{0,1,4,3,2:T(8,128)(2,1)S(1)} %copy-done.2, bf16[73,24,1440,1,1]{2,1,0,4,3:T(8,128)(2,1)S(1)} %bitcast.64), kind=kOutput, calls=%fused_computation.11 | convolution fusion | flops 969122304 | bytes 6271488 | tf_op jit(solution)/shard_map/bcnk,kdmp->dmpbnc/dot_general | solution.py:169
  10.1 0.5 maximum_bitcast_fusion
  10.6 2.4 %copy.12 = bf16[32,1,24,3,2,2,73]{6,5,4,3,2,0,1:T(2,128)(2,1)S(1)} copy(bf16[32,1,24,3,2,2,73]{6,0,2,5,3,1,4:T(8,128)(2,1)S(1)} %maximum_bitcast_fusion) | data formatting | bytes 2691072 | tf_op jit(solution)/shard_map/transpose | solution.py:174
  13.0 2.7 %reshape.67.send_ref = bf16[32,24,876]{2,1,0:T(8,128)(2,1)} reshape(bf16[32,1,24,3,2,2,73]{6,5,4,3,2,0,1:T(2,128)(2,1)S(1)} %copy.12) | data formatting | bytes 2691072 | tf_op jit(solution)/shard_map/reshape | solution.py:174
  15.7 38.8 %shard_map.59 = bf16[32,24,876]{2,1,0:T(8,128)(2,1)} custom-call(bf16[32,24,876]{2,1,0:T(8,128)(2,1)} %reshape.67.send_ref), custom_call_target="tpu_custom_call" | custom-call | tf_op jit(solution)/shard_map/pallas_call | solution.py:69
  54.5 6.8 %reshape.68 = bf16[4,8,24,3,2,2,73]{6,5,4,3,2,1,0:T(2,128)(2,1)S(1)} reshape(bf16[32,24,876]{2,1,0:T(8,128)(2,1)} %shard_map.59) | data formatting | bytes 2691072 | tf_op jit(solution)/shard_map/reshape.4
  61.3 3.2 %fusion = f32[720,2,73]{0,2,1:T(8,128)} fusion(f32[3]{0:T(128)S(1)} %compare_select_fusion, bf16[8,24,3,720,1,1,1]{3,1,0,6,5,4,2:T(8,128)(2,1)S(1)} %bitcast.57, bf16[4,8,24,3,2,2,73]{6,5,4,3,2,1,0:T(2,128)(2,1)S(1)} %reshape.68), kind=kOutput, calls=%fused_computation.1 | convolution fusion | flops 976249472 | bytes 2595468 | tf_op jit(solution)/shard_map/gtbnmfpc,tnml->mgbpfcl/dot_general | solution.py:178
  64.5 1.1 %reshape.70 = f32[146,720]{1,0:T(8,128)S(1)} reshape(f32[2,73,720]{2,1,0:T(8,128)} %bitcast.62) | data formatting | bytes 840960 | tf_op jit(solution)/shard_map/reshape | solution.py:192
  65.6 0.8 pad.9
  66.5 29.9 %shard_map.60 = f32[4,8,4,8,128]{4,3,2,1,0:T(8,128)} custom-call(f32[4,8,4,8,128]{4,3,2,1,0:T(8,128)} %bitcast.58), custom_call_target="tpu_custom_call" | custom-call | tf_op jit(solution)/shard_map/pallas_call | solution.py:143
  96.4 1.1 %slice.16 = f32[114,8,128]{2,1,0:T(8,128)S(1)} slice(f32[128,8,128]{2,1,0:T(8,128)} %bitcast.59), slice={[0:114], [0:8], [0:128]} | slice | bytes 933888 | tf_op jit(solution)/shard_map/slice | solution.py:197
  97.5 1.1 %copy.14 = f32[2,73,720]{2,0,1:T(2,128)} copy(f32[2,73,720]{2,1,0:T(8,128)S(1)} %div.16) | data formatting | bytes 840960
  98.6 0.1 add_log_fusion
  98.7 0.1 fusion.19
  98.8 0.5 broadcast_multiply_fusion
  (4 shorter events, 0.1 us)
Async XLA Ops:
  0.6 1.2 %copy-start = (bf16[192,3,720]{2,0,1:T(8,128)(2,1)S(1)}, bf16[192,3,720]{2,0,1:T(8,128)(2,1)}, u32[]{:S(2)}) copy-start(bf16[192,3,720]{2,0,1:T(8,128)(2,1)} %param.6) | copy-start | bytes 2488324
  1.8 5.5 %copy-start.1 = (bf16[1,73,24,1440]{3,2,1,0:T(8,128)(2,1)S(1)}, bf16[1,73,24,1440]{3,2,1,0:T(8,128)(2,1)}, u32[]{:S(2)}) copy-start(bf16[1,73,24,1440]{3,2,1,0:T(8,128)(2,1)} %param.5) | copy-start | bytes 15137284
  1.8 5.5 %copy-start.2 = (bf16[1440,32,3,2,1]{0,1,4,3,2:T(8,128)(2,1)S(1)}, bf16[1440,32,3,2,1]{0,1,4,3,2:T(8,128)(2,1)}, u32[]{:S(2)}) copy-start(bf16[1440,32,3,2,1]{0,1,4,3,2:T(8,128)(2,1)} %constant.41) | copy-start | bytes 1658884

commit v2 on v0

v2 whole, which is shorter than its diff:
```python
import functools
import math

import jax
import jax.numpy as jnp
import numpy as np
from jax import lax
from jax.experimental import pallas as pl
from jax.experimental.pallas import tpu as pltpu
from jax.sharding import PartitionSpec as P

MESH = pl.DeviceIdType.MESH
VMEM_SPEC = pl.BlockSpec(memory_space=pltpu.VMEM)


def fourier_table(lon_count, order_count):
    product_ids = np.arange(lon_count)[:, None] * np.arange(order_count)[None, :] % lon_count
    angles = np.float32(2.0 * math.pi / lon_count) * product_ids.astype(np.float32)
    inv_root = np.float32(1.0 / math.sqrt(lon_count))
    table = np.stack([np.cos(angles) * inv_root, -np.sin(angles) * inv_root], axis=2)
    return table.astype(jnp.bfloat16)


def greet_all(groups, bands):
    count = groups * bands
    me = lax.axis_index("batch") * bands + lax.axis_index("lat")
    barrier = pltpu.get_barrier_semaphore()

    @pl.loop(1, count)
    def _(step):
        peer = lax.rem(me + step, count)
        pl.semaphore_signal(
            barrier, inc=1, device_id=(peer // bands, lax.rem(peer, bands)), device_id_type=MESH
        )

    pl.semaphore_wait(barrier, count - 1)


def fused_kernel(groups, bands, scale, send_ref, basis_ref, spectra_ref, loss_ref,
                 arrived, powers, part, landed, other, pieces, send_sem, recv_sem, sums_sem, pair_sem):
    count = groups * bands
    my_group = lax.axis_index("batch")
    my_band = lax.axis_index("lat")
    me = my_group * bands + my_band
    per_dev, lat_total, degrees = basis_ref.shape
    lat_rows = lat_total // bands
    members = send_ref.shape[1] // lat_rows
    channels = spectra_ref.shape[1]
    width = 4 * channels
    greet_all(groups, bands)

    def device(peer):
        return (peer // bands, lax.rem(peer, bands))

    def block_copy(peer, slot):
        return pltpu.make_async_remote_copy(
            src_ref=send_ref.at[peer], dst_ref=arrived.at[slot],
            send_sem=send_sem.at[peer], recv_sem=recv_sem.at[slot],
            device_id=device(peer), device_id_type=MESH,
        )

    @pl.loop(1, count)
    def _(step):
        block_copy(lax.rem(me + step, count), me).start()

    arrived[me] = send_ref[me]
    powers[...] = jnp.zeros_like(powers)

    @pl.loop(1, groups + 1)
    def _(step):
        group = lax.rem(my_group + groups - step, groups)

        @pl.loop(0, bands)
        def _(band):
            source = group * bands + band

            @pl.when(source != me)
            def _():
                block_copy(source, source).wait_recv()

        for order in range(per_dev):
            start = order * width // 128 * 128
            stop = min(start + powers.shape[1], arrived.shape[2])
            weight = jnp.where(me * per_dev + order == 0, 1.0, 2.0).astype(jnp.float32)
            for member in range(members):
                rows = pl.ds(member * lat_rows, lat_rows)
                bands_in = [
                    arrived[group * bands + band, rows, start:stop].astype(jnp.float32)
                    for band in range(bands)
                ]
                fourier = jnp.concatenate(bands_in, axis=0).T.astype(jnp.bfloat16)
                coefficients = jnp.dot(
                    fourier, basis_ref[order], preferred_element_type=jnp.float32
                )
                powers[order, 0 : stop - start, 0:degrees] += weight * (coefficients * coefficients)

    row_tiles = -(-channels // 8)
    lane_tiles = powers.shape[2] // 128
    for field in range(2):
        for row in range(row_tiles):
            first = row * 8
            taken = min(8, channels - first)
            strip = jnp.zeros((taken, powers.shape[2]), jnp.float32)
            for order in range(per_dev):
                offset = order * width % 128 + field * 2 * channels + first
                for piece in range(2):
                    strip += powers[order, offset + piece * channels : offset + piece * channels + taken, :]
            for lane in range(lane_tiles):
                part[field, row * lane_tiles + lane, 0:taken, :] = strip[:, lane * 128 : (lane + 1) * 128]

    half = lax.rem(my_group, 2)
    mate = my_group + 1 - 2 * half
    pair = pltpu.make_async_remote_copy(
        src_ref=part.at[1 - half], dst_ref=landed,
        send_sem=pair_sem.at[0], recv_sem=pair_sem.at[1],
        device_id=(mate, my_band), device_id_type=MESH,
    )
    pair.start()
    pair.wait()
    part[half] = part[half] + landed[...]

    ranks = groups // 2 * bands
    rank = my_group // 2 * bands + my_band
    per_rank = part.shape[1] // ranks

    def tiles(owner):
        return pl.ds(owner * per_rank, per_rank)

    def rank_device(peer):
        return (peer // bands * 2 + half, lax.rem(peer, bands))

    def scatter(peer, slot):
        return pltpu.make_async_remote_copy(
            src_ref=part.at[half, tiles(peer)], dst_ref=pieces.at[slot],
            send_sem=sums_sem.at[0, peer], recv_sem=sums_sem.at[1, slot],
            device_id=rank_device(peer), device_id_type=MESH,
        )

    def gather(peer, slot):
        return pltpu.make_async_remote_copy(
            src_ref=landed.at[tiles(rank)], dst_ref=landed.at[tiles(slot)],
            send_sem=sums_sem.at[2, peer], recv_sem=sums_sem.at[3, slot],
            device_id=rank_device(peer), device_id_type=MESH,
        )

    def start_all(make):
        @pl.loop(1, ranks)
        def _(step):
            make(lax.rem(rank + step, ranks), rank).start()

    def wait_all(make):
        @pl.loop(1, ranks)
        def _(step):
            peer = lax.rem(rank + step, ranks)
            make(peer, peer).wait_recv()
            make(peer, peer).wait_send()

    start_all(scatter)
    pieces[rank] = part[half, tiles(rank)]
    wait_all(scatter)
    landed[tiles(rank)] = jnp.sum(pieces[...], axis=0)
    start_all(gather)
    wait_all(gather)

    last = pltpu.make_async_remote_copy(
        src_ref=landed, dst_ref=other,
        send_sem=pair_sem.at[2], recv_sem=pair_sem.at[3],
        device_id=(mate, my_band), device_id_type=MESH,
    )
    last.start()
    last.wait()
    part[half] = landed[...]
    part[1 - half] = other[...]

    for row in range(row_tiles):
        first = row * 8
        taken = min(8, channels - first)
        logs = []
        for field in range(2):
            strip = jnp.concatenate(
                [part[field, row * lane_tiles + lane] for lane in range(lane_tiles)], axis=1
            )
            strip = strip[0:taken, 0:degrees] * scale
            spectra_ref[field, first : first + taken, :] = strip
            logs.append(jnp.log(strip + 1e-06))
        gap = logs[0] - logs[1]
        loss_ref[first : first + taken, :] = jnp.sum(gap * gap, axis=1, keepdims=True) / degrees

    @pl.loop(1, count)
    def _(step):
        peer = lax.rem(me + step, count)
        block_copy(peer, peer).wait_send()


def fused(groups, bands, scale, channels, blocks, basis):
    count = groups * bands
    ranks = groups // 2 * bands
    degrees = basis.shape[2]
    lanes = -(-degrees // 128) * 128
    tiles = -(-channels // 8) * (lanes // 128)
    per_rank = -(-tiles // ranks)
    window = -(-(4 * channels + 127) // 128) * 128
    return pl.pallas_call(
        functools.partial(fused_kernel, groups, bands, scale),
        out_shape=(
            jax.ShapeDtypeStruct((2, channels, degrees), jnp.float32),
            jax.ShapeDtypeStruct((channels, 1), jnp.float32),
        ),
        in_specs=[VMEM_SPEC, VMEM_SPEC],
        out_specs=(VMEM_SPEC, VMEM_SPEC),
        scratch_shapes=[
            pltpu.VMEM(blocks.shape, blocks.dtype),
            pltpu.VMEM((basis.shape[0], window, lanes), jnp.float32),
            pltpu.VMEM((2, per_rank * ranks, 8, 128), jnp.float32),
            pltpu.VMEM((per_rank * ranks, 8, 128), jnp.float32),
            pltpu.VMEM((per_rank * ranks, 8, 128), jnp.float32),
            pltpu.VMEM((ranks, per_rank, 8, 128), jnp.float32),
            pltpu.SemaphoreType.DMA((count,)),
            pltpu.SemaphoreType.DMA((count,)),
            pltpu.SemaphoreType.DMA((4, ranks)),
            pltpu.SemaphoreType.DMA((4,)),
        ],
        compiler_params=pltpu.CompilerParams(
            collective_id=0, has_side_effects=True, vmem_limit_bytes=60 * 1024 * 1024
        ),
    )(blocks, basis)


def body(predicted, target, legendre_basis):
    groups = lax.axis_size("batch")
    bands = lax.axis_size("lat")
    count = groups * bands
    per_dev = legendre_basis.shape[1]
    members, channels, lat_rows, lon_count = predicted.shape
    order_count = per_dev * count
    table = jnp.asarray(fourier_table(lon_count, order_count))
    table = table.reshape(lon_count, count, per_dev, 2)

    def transform(field_in):
        return jnp.einsum(
            "bcnk,kdmp->dmpbnc", field_in, table, preferred_element_type=jnp.float32
        ).astype(jnp.bfloat16)

    blocks = jnp.stack([transform(predicted), transform(target)], axis=2)
    blocks = blocks.transpose(0, 4, 5, 1, 2, 3, 6).reshape(count, members * lat_rows, -1)
    scale = 1.0 / (members * groups * order_count)
    spectra, loss = fused(
        groups, bands, scale, channels, blocks, legendre_basis.transpose(1, 0, 2)
    )
    return (spectra, loss.reshape(channels))


def solution(mesh):
    placed = (
        P("batch", None, "lat", None),
        P("batch", None, "lat", None),
        P(None, ("batch", "lat"), None),
    )
    return jax.shard_map(body, mesh=mesh, in_specs=placed, out_specs=(P(), P()), check_vma=False)
```

time: 212 us -> 79.2 us (0.37)
  waiting for transfers between devices: 160 us -> 0 us
  Pallas kernels: 0 us -> 61 us
  between operations: 13.8 us -> 0.7 us
  starting transfers between devices: 7.66 us -> 0 us
  matrix products: 15.4 us -> 8.21 us
  other arithmetic: 7.07 us -> 1.94 us
    psum x2 -> x0, waiting for transfers between devices: 106 us -> none  [the longest x1 71.4 us: body(): energy = lax.psum(partial_value, 'lat')]
    pallas_call x0 -> x1, Pallas kernels: none -> 61 us  [fused(): pl.pallas_call(functools.partial(fused_kernel, groups, bands, scale), out...]
    all_to_all x1 -> x0, waiting for transfers between devices: 53.6 us -> none  [body(): lax.all_to_all(fourier, 'lat', split_axis=3, concat_axis=7, tiled=True)]
    all_to_all x1 -> x0, starting transfers between devices: 7.55 us -> none  [body(): lax.all_to_all(fourier, 'lat', split_axis=3, concat_axis=7, tiled=True)]
    dot_general x3 -> x2, matrix products: 15.4 us -> 8.21 us  [transform(): jnp.einsum('bcnk,kdmp->dmpbnc', field_in, table, preferred_element_type=j...]
    another operation x2 -> x0, other arithmetic: 3.1 us -> none
    reshape x0 -> x1, local copies, waits for them, and re-layouts: none -> 2.49 us  [body(): blocks.transpose(0, 4, 5, 1, 2, 3, 6).reshape(count, members * lat_rows, -1)]
    transpose x0 -> x1, local copies, waits for them, and re-layouts: none -> 2.43 us  [body(): blocks.transpose(0, 4, 5, 1, 2, 3, 6).reshape(count, members * lat_rows, -1)]
  transfers between devices with their start and end apart: 4 -> 0, of which waited for: 3 -> 0; matrix products, arithmetic and copies ran while one was open for 9% -> 0% of each run, Pallas kernels for 0% -> 0%
where the time goes in v2:
time: 79.2 us; the launch traced here: 78.9 us
  Pallas kernels  61 us (77%)
  matrix products  8.21 us (10%)
  local copies, waits for them, and re-layouts  7.07 us (9%)
  other arithmetic  1.94 us (2%)
    pallas_call x1, Pallas kernels, fused(): pl.pallas_call(functools.partial(fused_kernel, groups, bands, scale), out...  61 us
    dot_general x2, matrix products, transform(): jnp.einsum('bcnk,kdmp->dmpbnc', field_in, table, preferred_element_type=j...  8.21 us
    reshape x1, local copies, waits for them, and re-layouts, body(): blocks.transpose(0, 4, 5, 1, 2, 3, 6).reshape(count, members * lat_rows, -1)  2.49 us
    transpose x1, local copies, waits for them, and re-layouts, body(): blocks.transpose(0, 4, 5, 1, 2, 3, 6).reshape(count, members * lat_rows, -1)  2.43 us
    unnamed x5, local copies, waits for them, and re-layouts  2.15 us

profile of v2, /device:TPU:0, one launch (start us, length us, event | category | flops | bytes accessed | tf_op | source)
XLA Modules:
  0.0 78.9 jit_solution(9205946306672904662)
XLA Ops:
  0.6 0.0 copy-start
  0.6 0.0 copy-start.1
  0.7 5.5 %fusion.13 = bf16[32,3,1,2,1,24,73]{6,0,5,3,1,4,2:T(8,128)(2,1)S(1)} fusion(bf16[1440,32,3,2,1]{0,1,4,3,2:T(8,128)(2,1)} %constant.7, bf16[73,24,1440,1,1]{2,1,0,4,3:T(8,128)(2,1)} %bitcast.29), kind=kOutput, calls=%fused_computation.8 | convolution fusion | flops 969122304 | bytes 6271488 | tf_op jit(solution)/shard_map/bcnk,kdmp->dmpbnc/dot_general | solution.py:240
  6.2 0.0 copy-done
  6.2 0.0 copy-done.1
  6.2 2.7 %fusion.10 = bf16[32,3,1,2,1,24,73]{6,0,5,3,1,4,2:T(8,128)(2,1)S(1)} fusion(bf16[1440,32,3,2,1]{0,1,4,3,2:T(8,128)(2,1)S(1)} %copy-done.1, bf16[73,24,1440,1,1]{2,1,0,4,3:T(8,128)(2,1)S(1)} %bitcast.30), kind=kOutput, calls=%fused_computation.7 | convolution fusion | flops 969122304 | bytes 6271488 | tf_op jit(solution)/shard_map/bcnk,kdmp->dmpbnc/dot_general | solution.py:240
  8.9 0.5 maximum_bitcast_fusion
  9.4 2.4 %copy.12 = bf16[32,1,24,3,2,2,73]{6,5,4,3,2,0,1:T(2,128)(2,1)S(1)} copy(bf16[32,1,24,3,2,2,73]{6,0,2,5,3,1,4:T(8,128)(2,1)S(1)} %maximum_bitcast_fusion) | data formatting | bytes 2691072 | tf_op jit(solution)/shard_map/transpose | solution.py:245
  11.9 2.5 %reshape.26.send_ref = bf16[32,24,876]{2,1,0:T(8,128)(2,1)} reshape(bf16[32,1,24,3,2,2,73]{6,5,4,3,2,0,1:T(2,128)(2,1)S(1)} %copy.12) | data formatting | bytes 2691072 | tf_op jit(solution)/shard_map/reshape | solution.py:245
  14.4 61.0 %shard_map.59 = (f32[2,73,720]{2,1,0:T(8,128)}, f32[73,1]{1,0:T(8,128)}) custom-call(bf16[32,24,876]{2,1,0:T(8,128)(2,1)} %reshape.26.send_ref, bf16[3,192,720]{2,1,0:T(8,128)(2,1)} %bitcast.28), custom_call_target="tpu_custom_call" | custom-call | tf_op jit(solution)/shard_map/pallas_call | solution.py:203
  75.4 2.1 %copy.13 = f32[2,73,720]{2,0,1:T(2,128)} copy(f32[2,73,720]{2,1,0:T(8,128)} %get-tuple-element.8) | data formatting | bytes 840960
  77.5 1.4 %reduce = f32[73]{0:T(128)} reduce(f32[73,1]{1,0:T(8,128)} %get-tuple-element.5, f32[]{:T(128)} %constant.8), dimensions={1}, to_apply=%get-tuple-element.5.reduce_sub_computation | reduce | bytes 588 | tf_op jit(solution)/shard_map/pallas_call | solution.py:203
Async XLA Ops:
  0.6 5.5 %copy-start = (bf16[1,73,24,1440]{3,2,1,0:T(8,128)(2,1)S(1)}, bf16[1,73,24,1440]{3,2,1,0:T(8,128)(2,1)}, u32[]{:S(2)}) copy-start(bf16[1,73,24,1440]{3,2,1,0:T(8,128)(2,1)} %param.5) | copy-start | bytes 15137284
  0.6 5.5 %copy-start.1 = (bf16[1440,32,3,2,1]{0,1,4,3,2:T(8,128)(2,1)S(1)}, bf16[1440,32,3,2,1]{0,1,4,3,2:T(8,128)(2,1)}, u32[]{:S(2)}) copy-start(bf16[1440,32,3,2,1]{0,1,4,3,2:T(8,128)(2,1)} %constant.7) | copy-start | bytes 1658884
